TPU v7x, 32 devices: a whole 2x2x4 slice. The times are simulated.
32 devices in a mesh: groups: 2 (over x), seq: 16 (over z, y, core).
Axes of the slice: x: 2, y: 2, z: 4, core: 2. Of those that a mesh axis runs over, the one named last changes fastest.
Arguments:
- prefill_keys: bfloat16 [128, 4096, 128], P(('groups', 'seq')), parts along dimension 0, may hold values from -4 to 4
- prefill_values: bfloat16 [128, 4096, 128], P(('groups', 'seq')), parts along dimension 0, may hold values from -6 to 6
- window_queries: bfloat16 [128, 8, 256, 128], P(('groups', 'seq')), parts along dimension 0, may hold values from -48 to 48
- step_queries: bfloat16 [128, 2, 8, 128], P('groups'), parts along dimension 0, may hold values from -48 to 48
- new_keys: bfloat16 [128, 2, 128], P('groups'), parts along dimension 0, may hold values from -24 to 24
- new_values: bfloat16 [128, 2, 128], P('groups'), parts along dimension 0, may hold values from -6 to 6
- lengths: int32 [16], P('groups'), parts along dimension 0, may hold values from 2048 to 4096
- keep_mask: int32 [16, 32], P('groups'), parts along dimension 0, may hold values from 0 to 1, as said below
Outputs:
- cache_keys: bfloat16 [128, 4096, 128], P('groups', 'seq'), parts along dimension 0
- cache_values: bfloat16 [128, 4096, 128], P('groups', 'seq'), parts along dimension 0
- attended: bfloat16 [128, 2, 8, 128], P('groups'), parts along dimension 0
- block_scores: float32 [128, 32], P('groups', 'seq'), parts along dimension 0
There are 2 independent parts, one for each index of `groups`. A program takes and returns all parts, laid end to end along the dimension named above; each array names one. Nothing has to cross between parts.
Inputs may be any that keep to these rules, and one draw needn't show every extreme that they name: `keep_mask`: 1 keeps a block, 0 drops it; block 0 of every sequence is kept.
All inputs are finite; a program needn't handle non-finite values.
Results may differ from a plain program's by a relative error of at most 0.0055.
Values may be sent and summed in bfloat16 or wider, within the bound.
No kernel may reach another device: no remote copies, remote signals or barrier semaphores. Data moves between devices by JAX's collectives and lax.ppermute only.
A program may use at most 128 MiB of HBM per device.

v0:
```python
import math

import jax
import jax.numpy as jnp
from jax import lax
from jax.sharding import PartitionSpec as P

KVH = 8
GROUP = 8
BLOCK = 128


def window_mass(prefill_keys, window_queries, lengths, keep_mask, first_pair):
    pair_count, token_count, head_width = prefill_keys.shape
    block_count = keep_mask.shape[1]
    window_size = window_queries.shape[2]
    rows_pair = window_queries.shape[1] * window_size
    rows_block = math.gcd(rows_pair, 512)
    per_pair = rows_pair // rows_block
    flat_rows = window_queries.reshape(pair_count * per_pair, rows_block, head_width)
    scaling = 1.0 / math.sqrt(head_width)
    position = jnp.arange(token_count, dtype=jnp.int32)

    def one_block(block_index):
        pair_local = block_index // per_pair
        seq_id = (first_pair + pair_local) // KVH
        scores = (
            lax.dot_general(
                flat_rows[block_index],
                prefill_keys[pair_local],
                (((1,), (1,)), ((), ())),
                preferred_element_type=jnp.float32,
            )
            * scaling
        )
        row_offset = block_index % per_pair * rows_block + jnp.arange(rows_block, dtype=jnp.int32)
        query_pos = lengths[seq_id] - window_size + row_offset % window_size
        kept_tokens = jnp.broadcast_to(
            keep_mask[seq_id][:, None] > 0, (block_count, BLOCK)
        ).reshape(token_count)
        visible = kept_tokens[None, :] & (position[None, :] <= query_pos[:, None])
        scores = jnp.where(visible, scores, -jnp.inf)
        highest = jnp.max(scores, axis=1, keepdims=True)
        weights = jnp.exp(scores - highest)
        probability = weights / jnp.sum(weights, axis=1, keepdims=True)
        return jnp.sum(probability, axis=0).reshape(block_count, BLOCK).sum(axis=1)

    block_parts = lax.map(one_block, jnp.arange(pair_count * per_pair, dtype=jnp.int32))
    return block_parts.reshape(pair_count, per_pair, block_count).sum(axis=1) / GROUP


def select_rows(small_table, seq_ids):
    matches = seq_ids[:, None] == jnp.arange(small_table.shape[0], dtype=jnp.int32)[None, :]
    return jnp.sum(jnp.where(matches[:, :, None], small_table[None, :, :], 0), axis=1)


def step_scores(cache_part, queries_here, new_here, lengths, keep_mask, first_pair):
    pair_count, token_count, head_width = cache_part.shape
    step_count = queries_here.shape[1]
    group_size = queries_here.shape[2]
    query_rows = queries_here.reshape(pair_count, step_count * group_size, head_width)
    scaling = 1.0 / math.sqrt(head_width)
    scores = (
        jnp.einsum("pqd,ptd->pqt", query_rows, cache_part, preferred_element_type=jnp.float32)
        * scaling
    )
    seq_ids = (first_pair + jnp.arange(pair_count, dtype=jnp.int32)) // KVH
    block_count = token_count // BLOCK
    kept_blocks = select_rows(keep_mask, seq_ids) > 0
    kept_tokens = jnp.broadcast_to(
        kept_blocks[:, :, None], (pair_count, block_count, BLOCK)
    ).reshape(pair_count, token_count)
    seq_length = select_rows(lengths[:, None], seq_ids)[:, 0]
    position = jnp.arange(token_count, dtype=jnp.int32)
    visible = kept_tokens & (position[None, :] < seq_length[:, None])
    scores = jnp.where(visible[:, None, :], scores, -jnp.inf)
    own_scores = (
        jnp.einsum("pqd,pjd->pqj", query_rows, new_here, preferred_element_type=jnp.float32)
        * scaling
    )
    row_step = jnp.arange(step_count * group_size, dtype=jnp.int32) // group_size
    own_visible = jnp.arange(step_count, dtype=jnp.int32)[None, :] <= row_step[:, None]
    own_scores = jnp.where(own_visible[None], own_scores, -jnp.inf)
    return (scores, own_scores)


def local_terms(scores, cache_vals, highest):
    weights = jnp.exp(scores - highest[:, :, None])
    total_mass = jnp.sum(weights, axis=2)
    summed = jnp.einsum(
        "pqt,ptd->pqd", weights.astype(jnp.bfloat16), cache_vals, preferred_element_type=jnp.float32
    )
    return (weights, total_mass, summed)


def finish(summed, total_mass, weights, highest, own_scores, new_vals):
    own_weights = jnp.exp(own_scores - highest[:, :, None])
    total_mass = total_mass + jnp.sum(own_weights, axis=2)
    summed = summed + jnp.einsum(
        "pqj,pjd->pqd",
        own_weights.astype(jnp.bfloat16),
        new_vals,
        preferred_element_type=jnp.float32,
    )
    pair_count, row_count, head_width = summed.shape
    attended = (
        (summed / total_mass[:, :, None])
        .astype(jnp.bfloat16)
        .reshape(pair_count, row_count // GROUP, GROUP, head_width)
    )
    token_count = weights.shape[2]
    new_mass = (
        jnp.sum(weights / total_mass[:, :, None], axis=1)
        .reshape(pair_count, token_count // BLOCK, BLOCK)
        .sum(axis=2)
        / GROUP
    )
    return (attended, new_mass)


def local(
    prefill_keys,
    prefill_values,
    window_queries,
    step_queries,
    new_keys,
    new_values,
    lengths,
    keep_mask,
):
    pair_count = prefill_keys.shape[0]
    first_pair = lax.axis_index("seq") * pair_count
    prior_mass = window_mass(prefill_keys, window_queries, lengths, keep_mask, first_pair).astype(
        jnp.bfloat16
    )
    cache_keys, cache_values, prior_tokens = (
        lax.all_to_all(prefill_keys, "seq", split_axis=1, concat_axis=0, tiled=True),
        lax.all_to_all(prefill_values, "seq", split_axis=1, concat_axis=0, tiled=True),
        lax.all_to_all(prior_mass, "seq", split_axis=1, concat_axis=0, tiled=True),
    )
    queries_here = lax.dynamic_slice_in_dim(step_queries, first_pair, pair_count, 0)
    new_keys_here = lax.dynamic_slice_in_dim(new_keys, first_pair, pair_count, 0)
    new_values_here = lax.dynamic_slice_in_dim(new_values, first_pair, pair_count, 0)
    scores, own_scores = step_scores(
        prefill_keys, queries_here, new_keys_here, lengths, keep_mask, first_pair
    )
    highest = jnp.maximum(jnp.max(scores, axis=2), jnp.max(own_scores, axis=2))
    weights, total_mass, summed = local_terms(scores, prefill_values, highest)
    attended_here, mass_here = finish(
        summed, total_mass, weights, highest, own_scores, new_values_here
    )
    attended = lax.all_gather(attended_here, "seq", axis=0, tiled=True)
    new_mass = lax.all_to_all(mass_here, "seq", split_axis=1, concat_axis=0, tiled=True)
    block_scores = prior_tokens.astype(jnp.float32) + new_mass
    return (cache_keys, cache_values, attended, block_scores)


def solution(mesh):
    placed = (
        P(("groups", "seq"), None, None),
        P(("groups", "seq"), None, None),
        P(("groups", "seq"), None, None, None),
        P("groups", None, None, None),
        P("groups", None, None),
        P("groups", None, None),
        P("groups"),
        P("groups", None),
    )
    return jax.shard_map(
        local,
        mesh=mesh,
        in_specs=placed,
        out_specs=(
            P("groups", "seq", None),
            P("groups", "seq", None),
            P("groups", None, None, None),
            P("groups", "seq"),
        ),
        check_vma=False,
    )
```

profile of v0, /device:TPU:11, one launch (start us, length us, event | category | flops | bytes accessed | tf_op | source)
XLA Modules:
  0.0 480.5 jit_solution(5911037382524738119)
XLA Ops:
  0.7 232.3 %while.14 = (s32[]{:T(128)}, f32[16,32]{1,0:T(8,128)S(1)}, s32[16]{0:T(128)S(1)}, s32[]{:T(128)}, s32[8,32]{1,0:T(8,128)}, /*index=5*/s32[8]{0:T(128)}, bf16[16,...) while((s32[]{:T(128)}, f32[16,32]{1,0:T(8,128)S(1)}, ...), condition=%wide.region_11.12_spmd.clone, body=%wide.region_6.11_spmd.clone.sunk | while | flops 557848064 | bytes 26402040 | solution.py:48
  5.2 1.2 dynamic_slice.95
  7.9 4.0 fusion.44
  11.9 1.3 fusion.45
  13.1 1.9 divide_reduce_fusion.3
  19.7 1.2 dynamic_slice.95
  22.4 4.0 fusion.44
  26.4 1.3 fusion.45
  27.7 1.9 divide_reduce_fusion.3
  36.9 4.0 fusion.44
  40.9 1.3 fusion.45
  42.2 1.9 divide_reduce_fusion.3
  51.5 4.0 fusion.44
  55.4 1.3 fusion.45
  56.7 1.9 divide_reduce_fusion.3
  63.3 1.2 dynamic_slice.95
  66.0 4.0 fusion.44
  69.9 1.3 fusion.45
  71.2 1.9 divide_reduce_fusion.3
  80.5 4.0 fusion.44
  84.5 1.3 fusion.45
  85.7 1.9 divide_reduce_fusion.3
  95.0 4.0 fusion.44
  99.0 1.3 fusion.45
  100.3 1.9 divide_reduce_fusion.3
  109.5 4.0 fusion.44
  113.5 1.3 fusion.45
  114.8 1.9 divide_reduce_fusion.3
  124.0 4.0 fusion.44
  128.0 1.3 fusion.45
  129.3 1.9 divide_reduce_fusion.3
  138.6 4.0 fusion.44
  142.5 1.3 fusion.45
  143.8 1.9 divide_reduce_fusion.3
  153.1 4.0 fusion.44
  157.0 1.3 fusion.45
  158.3 1.9 divide_reduce_fusion.3
  167.6 4.0 fusion.44
  171.6 1.3 fusion.45
  172.8 1.9 divide_reduce_fusion.3
  182.1 4.0 fusion.44
  186.1 1.3 fusion.45
  187.4 1.9 divide_reduce_fusion.3
  196.6 4.0 fusion.44
  200.6 1.3 fusion.45
  201.9 1.9 divide_reduce_fusion.3
  211.1 4.0 fusion.44
  215.1 1.3 fusion.45
  216.4 1.9 divide_reduce_fusion.3
  225.7 4.0 fusion.44
  229.6 1.3 fusion.45
  230.9 1.9 divide_reduce_fusion.3
  233.7 6.5 %all-to-all-start.2 = ((bf16[4,16,2]{0,2,1:T(2,128)(2,1)}), bf16[4,16,2]{0,2,1:T(2,128)(2,1)S(1)}, u32[]{:S(2)}, u32[]{:S(2)}) async-start(bf16[4,16,2]{0,2,1:T(2,128)(2,1)} %bitcast.10), calls=%async_computation.2 | async-start | bytes 16384 | tf_op jit(solution)/shard_map/all_to_all | solution.py:139
  242.1 3.5 fusion.36
  247.9 6.0 %all-to-all-start.3 = ((f32[4,16,2]{0,2,1:T(2,128)}), f32[4,16,2]{0,2,1:T(2,128)S(1)}, u32[]{:S(2)}, u32[]{:S(2)}) async-start(f32[4,16,2]{0,2,1:T(2,128)} %bitcast.11), calls=%async_computation.3 | async-start | bytes 32768 | tf_op jit(solution)/shard_map/all_to_all | solution.py:153
  253.9 7.6 %copy.27 = bf16[4,4096,128]{2,0,1:T(4,128)(2,1)} copy(bf16[4,4096,128]{2,1,0:T(8,128)(2,1)} %param.11) | data formatting | bytes 8388608 | tf_op args[1]
  261.5 6.0 %all-to-all-start.1 = ((bf16[4,4096,128]{2,0,1:T(4,128)(2,1)}), bf16[4,4096,128]{2,0,1:T(4,128)(2,1)}, u32[]{:S(2)}, u32[]{:S(2)}) async-start(bf16[4,4096,128]{2,0,1:T(4,128)(2,1)} %copy.27), calls=%async_computation.1 | async-start | bytes 8388608 | tf_op jit(solution)/shard_map/all_to_all | solution.py:138
  267.5 7.6 %copy.25 = bf16[4,4096,128]{2,0,1:T(4,128)(2,1)} copy(bf16[4,4096,128]{2,1,0:T(8,128)(2,1)} %get-tuple-element.321) | data formatting | bytes 8388608 | tf_op args[0]
  275.1 82.7 %all-to-all-done.1 = bf16[4,4096,128]{2,0,1:T(4,128)(2,1)} async-done(((bf16[4,4096,128]{2,0,1:T(4,128)(2,1)}), bf16[4,4096,128]{2,0,1:T(4,128)(2,1)}, u32[]{:S(2)}, u32[]{:S(2)}) %all-to-all-start.1) | async-done | bytes 4194336 | tf_op jit(solution)/shard_map/all_to_all | solution.py:138
  357.7 7.0 %all-to-all-start = ((bf16[4,4096,128]{2,0,1:T(4,128)(2,1)}), bf16[4,4096,128]{2,0,1:T(4,128)(2,1)}, u32[]{:S(2)}, u32[]{:S(2)}) async-start(bf16[4,4096,128]{2,0,1:T(4,128)(2,1)} %copy.25), calls=%async_computation | async-start | bytes 8388608 | tf_op jit(solution)/shard_map/all_to_all | solution.py:137
  364.8 2.9 fusion.18
  368.6 99.9 %all_gather.3 = bf16[64,2,8,128]{3,2,1,0:T(8,128)(2,1)S(1)} all-gather(bf16[4,2,8,128]{3,2,1,0:T(8,128)(2,1)S(1)} %fusion.14), channel_id=1, replica_groups=mesh['groups'=2,'seq'=16] {'seq'}, dimensions={0}, use_global_device_ids=true | all-gather | bytes 278528 | tf_op jit(solution)/shard_map/all_gather | solution.py:152
  469.1 5.3 %copy.28 = bf16[16,4,256,128]{3,2,1,0:T(8,128)(2,1)} copy(bf16[16,4,256,128]{3,1,2,0:T(4,128)(2,1)} %bitcast.4) | data formatting | bytes 8388608 | tf_op jit(solution)/shard_map/all_to_all | solution.py:138
  474.5 5.3 %copy.26 = bf16[16,4,256,128]{3,2,1,0:T(8,128)(2,1)} copy(bf16[16,4,256,128]{3,1,2,0:T(4,128)(2,1)} %bitcast.1) | data formatting | bytes 8388608 | tf_op jit(solution)/shard_map/all_to_all | solution.py:137
  (142 shorter events, 47.6 us)
Async XLA Ops:
  0.6 241.4 %copy-start = (bf16[64,2,8,128]{3,2,1,0:T(8,128)(2,1)S(1)}, bf16[64,2,8,128]{3,2,1,0:T(8,128)(2,1)}, u32[]{:S(2)}) copy-start(bf16[64,2,8,128]{3,2,1,0:T(8,128)(2,1)} %param.13) | copy-start | bytes 786436
  233.7 14.2 %all-to-all-start.2 = ((bf16[4,16,2]{0,2,1:T(2,128)(2,1)}), bf16[4,16,2]{0,2,1:T(2,128)(2,1)S(1)}, u32[]{:S(2)}, u32[]{:S(2)}) async-start(bf16[4,16,2]{0,2,1:T(2,128)(2,1)} %bitcast.10), calls=%async_computation.2 | async-start | bytes 16384 | tf_op jit(solution)/shard_map/all_to_all | solution.py:139
  247.9 13.6 %all-to-all-start.3 = ((f32[4,16,2]{0,2,1:T(2,128)}), f32[4,16,2]{0,2,1:T(2,128)S(1)}, u32[]{:S(2)}, u32[]{:S(2)}) async-start(f32[4,16,2]{0,2,1:T(2,128)} %bitcast.11), calls=%async_computation.3 | async-start | bytes 32768 | tf_op jit(solution)/shard_map/all_to_all | solution.py:153
  261.5 96.2 %all-to-all-start.1 = ((bf16[4,4096,128]{2,0,1:T(4,128)(2,1)}), bf16[4,4096,128]{2,0,1:T(4,128)(2,1)}, u32[]{:S(2)}, u32[]{:S(2)}) async-start(bf16[4,4096,128]{2,0,1:T(4,128)(2,1)} %copy.27), calls=%async_computation.1 | async-start | bytes 8388608 | tf_op jit(solution)/shard_map/all_to_all | solution.py:138
  357.7 116.7 %all-to-all-start = ((bf16[4,4096,128]{2,0,1:T(4,128)(2,1)}), bf16[4,4096,128]{2,0,1:T(4,128)(2,1)}, u32[]{:S(2)}, u32[]{:S(2)}) async-start(bf16[4,4096,128]{2,0,1:T(4,128)(2,1)} %copy.25), calls=%async_computation | async-start | bytes 8388608 | tf_op jit(solution)/shard_map/all_to_all | solution.py:137
where the time goes:
time: 483 us; the launch traced here: 481 us
  blocking collectives  99.9 us (21%)
  waiting for transfers between devices  82.7 us (17%)
  loops' own time  73.9 us (15%)
  matrix products  71.5 us (15%)
  other arithmetic  66.7 us (14%)
  local copies, waits for them, and re-layouts  59.6 us (12%)
  starting transfers between devices  25.5 us (5%)
    all_gather x1, blocking collectives, local(): attended = lax.all_gather(attended_here, 'seq', axis=0, tiled=True)  99.9 us
    all_to_all x1, waiting for transfers between devices, local(): lax.all_to_all(prefill_values, 'seq', split_axis=1, concat_axis=0, tiled=...  82.7 us
    another operation x1, loops' own time, window_mass(): lax.map(one_block, jnp.arange(pair_count * per_pair, dtype=jnp.int32))  73.9 us
    dot_general x16, matrix products, one_block(): lax.dot_general(flat_rows[block_index], prefill_keys[pair_local], (((1,),...  63.4 us
    reduce_sum x32, other arithmetic, one_block(): return jnp.sum(probability, axis=0).reshape(block_count, BLOCK).sum(axis=1)  32.1 us
    reduce_sum x16, other arithmetic, one_block(): probability = weights / jnp.sum(weights, axis=1, keepdims=True)  20.6 us
    dynamic_slice x16, local copies, waits for them, and re-layouts, one_block(): query_pos = lengths[seq_id] - window_size + row_offset % window_size  19.9 us
    unnamed x6, local copies, waits for them, and re-layouts  15.9 us
  transfers between devices with their start and end apart: 4, of which 1 were waited for; matrix products, arithmetic and copies ran while one was open for 7% of the time, Pallas kernels for 0%

commit v1 on v0

v1 whole, which is shorter than its diff:
```python
import functools
import math

import jax
import jax.numpy as jnp
from jax import lax
from jax.experimental import pallas as pl
from jax.experimental.pallas import tpu as pltpu
from jax.sharding import PartitionSpec as P

KVH = 8
GROUP = 8
BLOCK = 128
HIDDEN = -1e30
ROWS = 256
CHUNK = 512


def window_kernel(lengths_ref, query_ref, key_ref, bias_ref, ones_ref, sum_ref, score_ref, *, window_size):
    step = pl.program_id(1)
    token_count, head_width = key_ref.shape[1:]
    row_count = query_ref.shape[1]
    scaling = math.log2(math.e) / math.sqrt(head_width)
    query_rows = query_ref[0]
    row_offset = lax.broadcasted_iota(jnp.int32, (row_count, 1), 0) + step * row_count
    query_pos = lengths_ref[pl.program_id(0)] - window_size + row_offset % window_size
    position = lax.broadcasted_iota(jnp.int32, (1, CHUNK), 1)
    peak = jnp.full((row_count, BLOCK), HIDDEN, jnp.float32)
    for first in range(0, token_count, CHUNK):
        scores = lax.dot_general(
            query_rows,
            key_ref[0, first : first + CHUNK, :],
            (((1,), (1,)), ((), ())),
            preferred_element_type=jnp.float32,
        )
        scores = scores * scaling + bias_ref[0, :, first : first + CHUNK]
        scores = jnp.where(position <= query_pos - first, scores, HIDDEN)
        score_ref[:, first : first + CHUNK] = scores
        for lane in range(0, CHUNK, BLOCK):
            peak = jnp.maximum(peak, scores[:, lane : lane + BLOCK])
    highest = jnp.max(peak, axis=1, keepdims=True)
    masses = jnp.zeros((row_count, ones_ref.shape[1]), jnp.float32)
    for first in range(0, token_count, CHUNK):
        weights = jnp.exp2(score_ref[:, first : first + CHUNK] - highest).astype(jnp.bfloat16)
        masses = masses + jnp.dot(
            weights, ones_ref[first : first + CHUNK, :], preferred_element_type=jnp.float32
        )
    total = jnp.sum(masses, axis=1, keepdims=True)
    result = jnp.sum(masses / total, axis=0, keepdims=True)

    @pl.when(step == 0)
    def _():
        sum_ref[...] = jnp.zeros_like(sum_ref)

    sum_ref[0] = sum_ref[0] + result


def window_mass(prefill_keys, window_queries, lengths_here, kept_blocks):
    pair_count, token_count, head_width = prefill_keys.shape
    block_count = kept_blocks.shape[1]
    window_size = window_queries.shape[2]
    rows_pair = window_queries.shape[1] * window_size
    query_rows = window_queries.reshape(pair_count, rows_pair, head_width)
    bias = jnp.broadcast_to(
        jnp.where(kept_blocks > 0, 0.0, HIDDEN).astype(jnp.float32)[:, :, None],
        (pair_count, block_count, BLOCK),
    ).reshape(pair_count, 1, token_count)
    width = -(-block_count // BLOCK) * BLOCK
    ones = (
        jnp.arange(token_count, dtype=jnp.int32)[:, None] // BLOCK
        == jnp.arange(width, dtype=jnp.int32)[None, :]
    ).astype(jnp.bfloat16)
    sums = pl.pallas_call(
        functools.partial(window_kernel, window_size=window_size),
        grid_spec=pltpu.PrefetchScalarGridSpec(
            num_scalar_prefetch=1,
            grid=(pair_count, rows_pair // ROWS),
            in_specs=[
                pl.BlockSpec((1, ROWS, head_width), lambda p, s, _: (p, s, 0)),
                pl.BlockSpec((1, token_count, head_width), lambda p, s, _: (p, 0, 0)),
                pl.BlockSpec((1, 1, token_count), lambda p, s, _: (p, 0, 0)),
                pl.BlockSpec((token_count, width), lambda p, s, _: (0, 0)),
            ],
            out_specs=pl.BlockSpec((1, 1, width), lambda p, s, _: (p, 0, 0)),
            scratch_shapes=[pltpu.VMEM((ROWS, token_count), jnp.float32)],
        ),
        out_shape=jax.ShapeDtypeStruct((pair_count, 1, width), jnp.float32),
        compiler_params=pltpu.CompilerParams(dimension_semantics=("arbitrary", "arbitrary")),
        name="window_mass",
    )(lengths_here, query_rows, prefill_keys, bias, ones)
    return sums[:, 0, :block_count] / GROUP


def select_rows(small_table, seq_ids):
    matches = seq_ids[:, None] == jnp.arange(small_table.shape[0], dtype=jnp.int32)[None, :]
    return jnp.sum(jnp.where(matches[:, :, None], small_table[None, :, :], 0), axis=1)


def step_scores(cache_part, queries_here, new_here, seq_length, kept):
    pair_count, token_count, head_width = cache_part.shape
    step_count = queries_here.shape[1]
    group_size = queries_here.shape[2]
    query_rows = queries_here.reshape(pair_count, step_count * group_size, head_width)
    scaling = 1.0 / math.sqrt(head_width)
    scores = (
        jnp.einsum("pqd,ptd->pqt", query_rows, cache_part, preferred_element_type=jnp.float32)
        * scaling
    )
    block_count = token_count // BLOCK
    kept_blocks = kept > 0
    kept_tokens = jnp.broadcast_to(
        kept_blocks[:, :, None], (pair_count, block_count, BLOCK)
    ).reshape(pair_count, token_count)
    position = jnp.arange(token_count, dtype=jnp.int32)
    visible = kept_tokens & (position[None, :] < seq_length[:, None])
    scores = jnp.where(visible[:, None, :], scores, -jnp.inf)
    own_scores = (
        jnp.einsum("pqd,pjd->pqj", query_rows, new_here, preferred_element_type=jnp.float32)
        * scaling
    )
    row_step = jnp.arange(step_count * group_size, dtype=jnp.int32) // group_size
    own_visible = jnp.arange(step_count, dtype=jnp.int32)[None, :] <= row_step[:, None]
    own_scores = jnp.where(own_visible[None], own_scores, -jnp.inf)
    return (scores, own_scores)


def local_terms(scores, cache_vals, highest):
    weights = jnp.exp(scores - highest[:, :, None])
    total_mass = jnp.sum(weights, axis=2)
    summed = jnp.einsum(
        "pqt,ptd->pqd", weights.astype(jnp.bfloat16), cache_vals, preferred_element_type=jnp.float32
    )
    return (weights, total_mass, summed)


def finish(summed, total_mass, weights, highest, own_scores, new_vals):
    own_weights = jnp.exp(own_scores - highest[:, :, None])
    total_mass = total_mass + jnp.sum(own_weights, axis=2)
    summed = summed + jnp.einsum(
        "pqj,pjd->pqd",
        own_weights.astype(jnp.bfloat16),
        new_vals,
        preferred_element_type=jnp.float32,
    )
    pair_count, row_count, head_width = summed.shape
    attended = (
        (summed / total_mass[:, :, None])
        .astype(jnp.bfloat16)
        .reshape(pair_count, row_count // GROUP, GROUP, head_width)
    )
    token_count = weights.shape[2]
    new_mass = (
        jnp.sum(weights / total_mass[:, :, None], axis=1)
        .reshape(pair_count, token_count // BLOCK, BLOCK)
        .sum(axis=2)
        / GROUP
    )
    return (attended, new_mass)


def local(
    prefill_keys,
    prefill_values,
    window_queries,
    step_queries,
    new_keys,
    new_values,
    lengths,
    keep_mask,
):
    pair_count, token_count, head_width = prefill_keys.shape
    place = lax.axis_index("seq")
    first_pair = place * pair_count
    seq_ids = (first_pair + jnp.arange(pair_count, dtype=jnp.int32)) // KVH
    kept = select_rows(keep_mask, seq_ids)
    seq_length = select_rows(lengths[:, None], seq_ids)[:, 0]

    device_count = lax.axis_size("seq")
    width = token_count // device_count

    def by_target(cache):
        blocks = cache.reshape(pair_count, device_count, width, head_width).transpose(1, 0, 2, 3)
        return blocks.reshape(device_count, pair_count * width, head_width)

    def exchange(blocks):
        moved = lax.all_to_all(blocks, "seq", split_axis=0, concat_axis=0, tiled=True)
        return moved.reshape(device_count * pair_count, width, head_width)

    cache_keys = exchange(by_target(prefill_keys))
    prior_mass = window_mass(prefill_keys, window_queries, seq_length, kept).astype(jnp.bfloat16)
    value_blocks, prior_mass, cache_keys = lax.optimization_barrier(
        (by_target(prefill_values), prior_mass, cache_keys)
    )
    cache_values = exchange(value_blocks)
    queries_here = lax.dynamic_slice_in_dim(step_queries, first_pair, pair_count, 0)
    new_keys_here = lax.dynamic_slice_in_dim(new_keys, first_pair, pair_count, 0)
    new_values_here = lax.dynamic_slice_in_dim(new_values, first_pair, pair_count, 0)
    scores, own_scores = step_scores(prefill_keys, queries_here, new_keys_here, seq_length, kept)
    highest = jnp.maximum(jnp.max(scores, axis=2), jnp.max(own_scores, axis=2))
    weights, total_mass, summed = local_terms(scores, prefill_values, highest)
    attended_here, mass_here = finish(
        summed, total_mass, weights, highest, own_scores, new_values_here
    )
    attended = lax.all_gather(attended_here, "seq", axis=0, tiled=True)
    block_mass = prior_mass.astype(jnp.float32) + mass_here
    block_scores = lax.all_to_all(block_mass, "seq", split_axis=1, concat_axis=0, tiled=True)
    return (cache_keys, cache_values, attended, block_scores)


def solution(mesh):
    placed = (
        P(("groups", "seq"), None, None),
        P(("groups", "seq"), None, None),
        P(("groups", "seq"), None, None, None),
        P("groups", None, None, None),
        P("groups", None, None),
        P("groups", None, None),
        P("groups"),
        P("groups", None),
    )
    return jax.shard_map(
        local,
        mesh=mesh,
        in_specs=placed,
        out_specs=(
            P("groups", "seq", None),
            P("groups", "seq", None),
            P("groups", None, None, None),
            P("groups", "seq"),
        ),
        check_vma=False,
    )
```

time: 483 us -> 235 us (0.49)
  loops' own time: 73.9 us -> 0 us
  waiting for transfers between devices: 82.7 us -> 11 us
  Pallas kernels: 0 us -> 64.1 us
  matrix products: 71.5 us -> 8.08 us
  other arithmetic: 66.7 us -> 5.2 us
  local copies, waits for them, and re-layouts: 59.6 us -> 21.1 us
  starting transfers between devices: 25.5 us -> 12.4 us
  blocking collectives: 99.9 us -> 112 us
    another operation x1 -> x0, loops' own time: 73.9 us -> none  [window_mass(): lax.map(one_block, jnp.arange(pair_count * per_pair, dtype=jnp.int32))]
    all_to_all x4 -> x2, waiting for transfers between devices: 82.7 us -> 11 us  [exchange(): lax.all_to_all(blocks, 'seq', split_axis=0, concat_axis=0, tiled=True)]
    pallas_call x0 -> x1, Pallas kernels: none -> 64.1 us  [window_mass(): pl.pallas_call(functools.partial(window_kernel, window_size=window_size),...]
    dot_general x16 -> x0, matrix products: 63.4 us -> none  [one_block(): lax.dot_general(flat_rows[block_index], prefill_keys[pair_local], (((1,),...]
    reduce_sum x49 -> x0, other arithmetic: 52.6 us -> none  [the longest x32 32.1 us: one_block(): return jnp.sum(probability, axis=0).reshape(block_count, BLOCK).sum(axis=1)]
    dynamic_slice x32 -> x0, local copies, waits for them, and re-layouts: 29.3 us -> none  [the longest x16 19.9 us: one_block(): query_pos = lengths[seq_id] - window_size + row_offset % window_size]
    all_to_all x4 -> x2, starting transfers between devices: 25.5 us -> 12.4 us  [exchange(): lax.all_to_all(blocks, 'seq', split_axis=0, concat_axis=0, tiled=True)]
    all_to_all x0 -> x1, blocking collectives: none -> 11.8 us  [local(): lax.all_to_all(block_mass, 'seq', split_axis=1, concat_axis=0, tiled=True)]
  transfers between devices with their start and end apart: 4 -> 2, of which waited for: 1 -> 1; matrix products, arithmetic and copies ran while one was open for 7% -> 8% of each run, Pallas kernels for 0% -> 27%
where the time goes in v1:
time: 235 us; the launch traced here: 234 us
  blocking collectives  112 us (48%)
  Pallas kernels  64.1 us (27%)
  local copies, waits for them, and re-layouts  21.1 us (9%)
  starting transfers between devices  12.4 us (5%)
  waiting for transfers between devices  11 us (5%)
  matrix products  8.08 us (3%)
  other arithmetic  5.2 us (2%)
    all_gather x1, blocking collectives, local(): attended = lax.all_gather(attended_here, 'seq', axis=0, tiled=True)  99.9 us
    pallas_call x1, Pallas kernels, window_mass(): pl.pallas_call(functools.partial(window_kernel, window_size=window_size),...  64.1 us
    all_to_all x2, starting transfers between devices, exchange(): lax.all_to_all(blocks, 'seq', split_axis=0, concat_axis=0, tiled=True)  12.4 us
    all_to_all x1, blocking collectives, local(): lax.all_to_all(block_mass, 'seq', split_axis=1, concat_axis=0, tiled=True)  11.8 us
    all_to_all x2, waiting for transfers between devices, exchange(): lax.all_to_all(blocks, 'seq', split_axis=0, concat_axis=0, tiled=True)  11 us
    unnamed x13, local copies, waits for them, and re-layouts  10.2 us
    transpose x2, local copies, waits for them, and re-layouts, by_target(): cache.reshape(pair_count, device_count, width, head_width)  9.45 us
  transfers between devices with their start and end apart: 2, of which 1 were waited for; matrix products, arithmetic and copies ran while one was open for 8% of the time, Pallas kernels for 27%

profile of v1, /device:TPU:11, one launch (start us, length us, event | category | flops | bytes accessed | tf_op | source)
XLA Modules:
  0.0 234.5 jit_solution(15203200065674994140)
XLA Ops:
  0.6 0.0 copy-start
  0.6 4.7 %copy.25 = bf16[16,4,256,128]{3,2,1,0:T(8,128)(2,1)} copy(bf16[16,4,256,128]{3,2,0,1:T(8,128)(2,1)} %bitcast.39) | data formatting | bytes 8388608 | tf_op jit(solution)/shard_map/transpose | solution.py:182
  5.4 6.6 %all-to-all-start = ((bf16[16,1024,128]{2,1,0:T(8,128)(2,1)}), bf16[16,1024,128]{2,1,0:T(8,128)(2,1)}, u32[]{:S(2)}, u32[]{:S(2)}) async-start(bf16[16,1024,128]{2,1,0:T(8,128)(2,1)} %bitcast.42), calls=%async_computation | async-start | bytes 8388608 | tf_op jit(solution)/shard_map/all_to_all | solution.py:186
  12.0 0.0 copy-start.3
  12.0 0.0 copy-start.1
  12.0 4.7 %copy.24 = bf16[16,4,256,128]{3,2,1,0:T(8,128)(2,1)} copy(bf16[16,4,256,128]{3,2,0,1:T(8,128)(2,1)} %bitcast.40) | data formatting | bytes 8388608 | tf_op jit(solution)/shard_map/transpose | solution.py:182
  16.7 0.0 copy-done.3
  16.7 0.7 select_reduce_fusion.1.lengths_ref
  17.4 0.1 iota_compare_fusion.2
  17.5 0.0 copy-done.1
  17.5 0.1 select_reduce_fusion
  17.6 0.0 copy-start.2
  17.6 2.7 %fusion.1.ones_ref = bf16[4096,128]{1,0:T(8,128)(2,1)} fusion(s32[4096]{0:T(1024)S(1)} %add_select_fusion), kind=kLoop, calls=%fused_computation.3 | loop fusion | flops 1048576 | bytes 1064960 | tf_op jit(solution)/shard_map/convert_element_type | solution.py:72
  20.3 0.7 broadcast_in_dim.101
  21.0 64.1 %window_mass.1 = f32[4,1,128]{2,1,0:T(1,128)} custom-call(s32[4]{0:T(128)} %select_reduce_fusion.1.lengths_ref, bf16[4,2048,128]{2,1,0:T(8,128)(2,1)} %bitcast.43, bf16[4,4096,128]{2,1,0:T(8,128)(2,1)} %key_ref.1, f32[4,1,4096]{2,1,0:T(1,128)} %bitcast.44, bf16[4096,128]{1,0:T(8,128)(2,1)} %fusion.1.ones_ref), custom_call_target="tpu_custom_call" | custom-call | tf_op jit(solution)/shard_map/window_mass/pallas_call | solution.py:73
  85.1 0.7 fusion.22
  85.8 0.0 copy-done
  85.8 0.8 fusion.30
  86.6 0.1 broadcast_bitcast_fusion
  86.7 0.0 copy-done.2
  86.7 0.1 fusion.11
  86.8 3.5 %fusion.29 = (f32[4,16]{1,0:T(4,128)S(1)}, f32[4,16,4096]{2,1,0:T(8,128)S(1)}) fusion(bf16[4,4096,128]{2,1,0:T(8,128)(2,1)} %key_ref.1, bf16[64,2,8,128]{3,2,1,0:T(8,128)(2,1)S(1)} %copy-done, s32[]{:T(128)S(6)} %select_n.70, pred[4,4096]{1,0:T(4,128)(4,1)S(1)} %fusion.11), kind=kOutput, calls=%fused_computation.59 | convolution fusion | flops 67895232 | bytes 5275908 | tf_op jit(solution)/shard_map/pqd,ptd->pqt/dot_general | solution.py:106
  90.4 0.3 fusion.6
  90.7 0.4 divide_reduce_fusion
  91.1 0.1 bitcast_reduce_fusion
  91.1 11.0 %all-to-all-done = bf16[16,1024,128]{2,1,0:T(8,128)(2,1)} async-done(((bf16[16,1024,128]{2,1,0:T(8,128)(2,1)}), bf16[16,1024,128]{2,1,0:T(8,128)(2,1)}, u32[]{:S(2)}, u32[]{:S(2)}) %all-to-all-start) | async-done | bytes 4194336 | tf_op jit(solution)/shard_map/all_to_all | solution.py:186
  102.2 0.1 copy.26
  102.3 11.8 %all_to_all.29 = f32[4,16,2]{0,2,1:T(2,128)S(1)} all-to-all(f32[4,16,2]{0,2,1:T(2,128)S(1)} %bitcast.47), channel_id=1, replica_groups=mesh['groups'=2,'seq'=16] {'seq'}, dimensions={1} | all-to-all | bytes 1024 | tf_op jit(solution)/shard_map/all_to_all | solution.py:206
  114.1 5.9 %all-to-all-start.1 = ((bf16[16,1024,128]{2,1,0:T(8,128)(2,1)}), bf16[16,1024,128]{2,1,0:T(8,128)(2,1)}, u32[]{:S(2)}, u32[]{:S(2)}) async-start(bf16[16,1024,128]{2,1,0:T(8,128)(2,1)} %bitcast.41), calls=%async_computation.1 | async-start | bytes 8388608 | tf_op jit(solution)/shard_map/all_to_all | solution.py:186
  120.0 2.9 %fusion.8 = f32[4,16,128]{2,1,0:T(8,128)S(1)} fusion(bf16[4,4096,128]{2,1,0:T(8,128)(2,1)} %param.9, f32[4,16,4096]{2,1,0:T(8,128)S(1)} %get-tuple-element.13, f32[4,16]{1,0:T(4,128)S(1)} %max.7), kind=kOutput, calls=%fused_computation.14 | convolution fusion | flops 67633152 | bytes 5275904 | tf_op jit(solution)/shard_map/pqt,ptd->pqd/dot_general | solution.py:130
  122.9 0.9 fusion.4
  123.8 99.9 %all_gather.3 = bf16[64,2,8,128]{3,2,1,0:T(8,128)(2,1)S(1)} all-gather(bf16[4,2,8,128]{3,2,1,0:T(8,128)(2,1)S(1)} %fusion.4), channel_id=1, replica_groups=mesh['groups'=2,'seq'=16] {'seq'}, dimensions={0}, use_global_device_ids=true | all-gather | bytes 278528 | tf_op jit(solution)/shard_map/all_gather | solution.py:204
  223.7 0.7 all_to_all.25
  224.3 0.0 all-to-all-done.1
  224.4 4.7 %copy.38 = bf16[64,256,128]{2,1,0:T(8,128)(2,1)} copy(bf16[64,256,128]{2,1,0:T(8,128)(2,1)} %bitcast.8) | data formatting | bytes 8388608
  229.1 4.7 %copy.39 = bf16[64,256,128]{2,1,0:T(8,128)(2,1)} copy(bf16[64,256,128]{2,1,0:T(8,128)(2,1)} %bitcast.9) | data formatting | bytes 8388608
  233.7 0.7 copy.40
  (11 shorter events, 0.1 us)
Async XLA Ops:
  0.6 85.2 %copy-start = (bf16[64,2,8,128]{3,2,1,0:T(8,128)(2,1)S(1)}, bf16[64,2,8,128]{3,2,1,0:T(8,128)(2,1)}, u32[]{:S(2)}) copy-start(bf16[64,2,8,128]{3,2,1,0:T(8,128)(2,1)} %param.11) | copy-start | bytes 786436
  5.4 96.8 %all-to-all-start = ((bf16[16,1024,128]{2,1,0:T(8,128)(2,1)}), bf16[16,1024,128]{2,1,0:T(8,128)(2,1)}, u32[]{:S(2)}, u32[]{:S(2)}) async-start(bf16[16,1024,128]{2,1,0:T(8,128)(2,1)} %bitcast.42), calls=%async_computation | async-start | bytes 8388608 | tf_op jit(solution)/shard_map/all_to_all | solution.py:186
  12.0 4.8 %copy-start.3 = (s32[8]{0:T(128)S(1)}, s32[8]{0:T(128)}, u32[]{:S(2)}) copy-start(s32[8]{0:T(128)} %param.14) | copy-start | bytes 100
  12.0 5.5 %copy-start.1 = (s32[8,32]{1,0:T(8,128)S(1)}, s32[8,32]{1,0:T(8,128)}, u32[]{:S(2)}) copy-start(s32[8,32]{1,0:T(8,128)} %param.15) | copy-start | bytes 3076
  17.6 69.1 %copy-start.2 = (s32[4]{0:T(128)S(1)}, s32[4]{0:T(128)}, u32[]{:S(2)}) copy-start(s32[4]{0:T(128)} %select_reduce_fusion.1.lengths_ref) | copy-start | bytes 52
  114.1 110.2 %all-to-all-start.1 = ((bf16[16,1024,128]{2,1,0:T(8,128)(2,1)}), bf16[16,1024,128]{2,1,0:T(8,128)(2,1)}, u32[]{:S(2)}, u32[]{:S(2)}) async-start(bf16[16,1024,128]{2,1,0:T(8,128)(2,1)} %bitcast.41), calls=%async_computation.1 | async-start | bytes 8388608 | tf_op jit(solution)/shard_map/all_to_all | solution.py:186
